TPU v7x, 32 devices: a whole 2x2x4 slice. The times are simulated.
32 devices in a mesh: gx: 4 (over z), gy: 4 (over x, core), gz: 2 (over y).
Axes of the slice: x: 2, y: 2, z: 4, core: 2. Of those that a mesh axis runs over, the one named last changes fastest.
Arguments:
- volume: int32 [32, 64, 256], P('gx', 'gy', 'gz'), may hold values from 0 to 255
- transfer_table: float32 [4, 256], replicated, may hold values from 0 to 1
- depth_rank: int32 [4], replicated, may hold values from 0 to 3, each once
- footprint: int32 [4, 4, 2, 4], P('gx', 'gy', 'gz'), may hold values from 0 to 128, as said below
Outputs:
- rendered: float32 [4, 64, 256], P(None, 'gy', 'gz')
Inputs may be any that keep to these rules, and one draw needn't show every extreme that they name: depth_rank holds each of 0 to 4 - 1 once. `footprint`: for every brick, entry 0 is below 8 and entry 1 above it, up to 16; entry 2 is below 64 and entry 3 above it, up to 128.
All inputs are finite; a program needn't handle non-finite values.
Results may differ from a plain program's by a relative error of at most 0.0003.
Values sent between devices are 32-bit elements; how exact they have to be, the bound alone decides.
A program may use at most 64 MiB of HBM per device.

v0:
```python
import jax
import jax.numpy as jnp
from jax import lax
from jax.sharding import PartitionSpec as P

light_x = 1.0 / 3.0
light_y = 2.0 / 3.0
light_z = 2.0 / 3.0


def with_halo(cells, sides, width):
    for axis, dim in sides:
        count = lax.axis_size(axis)
        ends = count - 1
        head = lax.slice_in_dim(cells, 0, width, axis=dim)
        tail = lax.slice_in_dim(cells, cells.shape[dim] - width, cells.shape[dim], axis=dim)
        cells = jnp.concatenate(
            [
                lax.ppermute(tail, axis, [(i, (i + 1) % count) for i in range(ends)]),
                cells,
                lax.ppermute(head, axis, [((i + 1) % count, i) for i in range(ends)]),
            ],
            axis=dim,
        )
    return cells


def shading(lower_plane, upper_plane, padded):
    grad_x = 0.5 * (upper_plane - lower_plane)
    grad_y = 0.5 * (padded[2:, 1:-1] - padded[:-2, 1:-1])
    grad_z = 0.5 * (padded[1:-1, 2:] - padded[1:-1, :-2])
    facing = jnp.abs(grad_x * light_x + grad_y * light_y + grad_z * light_z) / jnp.sqrt(
        1.0 + (grad_x * grad_x + grad_y * grad_y + grad_z * grad_z)
    )
    return 0.35 + 0.65 * facing


def composite(layers, depth_rank):
    order = jnp.argsort(depth_rank)
    ordered = jnp.take(layers, order, axis=0)

    def blend(state_pair, front_layer):
        colour, alpha = state_pair
        cover = 1.0 - alpha
        return ((colour + cover * front_layer[:3], alpha + cover * front_layer[3]), None)

    start_pair = (
        jnp.zeros((3,) + layers.shape[2:], jnp.float32),
        jnp.zeros(layers.shape[2:], jnp.float32),
    )
    (colour, alpha), unused = lax.scan(blend, start_pair, ordered)
    return jnp.concatenate([colour, alpha[None]], axis=0)


def on_device(volume, transfer_table, depth_rank, footprint):
    slab_depth, rows_here, cols_here = volume.shape
    columns = lax.axis_size("gx")
    extent = 4.0 / (slab_depth * columns)
    looked = jnp.take(transfer_table, volume, axis=1)
    density = looked[3]
    emission = looked[:3]
    padded = with_halo(density, (("gx", 0), ("gy", 1), ("gz", 2)), 1)

    def advance(state_pair, offset):
        colour, transmit = state_pair
        window = lax.dynamic_slice_in_dim(padded, offset, 3, 0)
        centre = window[1, 1:-1, 1:-1]
        shading_term = shading(window[0, 1:-1, 1:-1], window[2, 1:-1, 1:-1], window[1])
        emitted = lax.dynamic_index_in_dim(emission, offset, 1, keepdims=False) * shading_term
        sample_alpha = 1.0 - jnp.exp(-extent * centre)
        colour = colour + transmit * sample_alpha * emitted
        transmit = transmit * (1.0 - sample_alpha)
        return ((colour, transmit), None)

    start_pair = (
        jnp.zeros((3, rows_here, cols_here), jnp.float32),
        jnp.ones((rows_here, cols_here), jnp.float32),
    )
    (colour, transmit), unused = lax.scan(
        advance, start_pair, jnp.arange(slab_depth, dtype=jnp.int32)
    )
    rect = footprint[0, 0, 0]
    rows_local = jnp.arange(rows_here, dtype=jnp.int32)[:, None]
    cols_local = jnp.arange(cols_here, dtype=jnp.int32)[None, :]
    inside = (
        (rows_local >= rect[0])
        & (rows_local < rect[1])
        & (cols_local >= rect[2])
        & (cols_local < rect[3])
    )
    layer = jnp.concatenate([colour, (1.0 - transmit)[None]], axis=0)
    partial_value = jnp.where(inside[None], layer, 0.0)[None]
    layers = lax.all_gather(partial_value, "gx", axis=0, tiled=True)
    rendered = composite(layers, depth_rank)
    return rendered


def solution(mesh):
    placed = (P("gx", "gy", "gz"), P(), P(), P("gx", "gy", "gz", None))
    return jax.shard_map(
        on_device, mesh=mesh, in_specs=placed, out_specs=P(None, "gy", "gz"), check_vma=False
    )
```

profile of v0, /device:TPU:0, one launch (start us, length us, event | category | flops | bytes accessed | tf_op | source)
XLA Modules:
  0.0 137.6 jit_solution(11093514029266378517)
XLA Ops:
  0.0 0.9 compare_select_fusion
  0.9 0.9 compare_and_fusion
  1.8 0.8 copy.8
  2.6 54.5 %gather_fusion = f32[16384,4]{1,0:T(8,128)} fusion(f32[4,256]{0,1:T(8,128)S(1)} %copy.8, s32[16384]{0:T(1024)S(1)} %broadcast_clamp_fusion), kind=kCustom, calls=%fused_computation | custom fusion | bytes 589824 | tf_op jit(solution)/shard_map/jit(_take)/gather | solution.py:59
  57.1 5.2 %copy.9 = f32[8,16,128,4]{2,1,3,0:T(8,128)S(1)} copy(f32[8,16,128,4]{3,2,1,0:T(8,128)} %bitcast.81) | data formatting | bytes 524288 | tf_op jit(solution)/shard_map/jit(_take)/gather | solution.py:59
  62.4 5.0 %collective-permute-start = (f32[1,16,128]{2,1,0:T(8,128)S(1)}, f32[1,16,128]{2,1,0:T(8,128)S(1)}, u32[]{:S(2)}, u32[]{:S(2)}) collective-permute-start(f32[1,16,128]{2,1,0:T(8,128)S(1)} %get-tuple-element.194), channel_id=1, source_target_pairs={{0,8},{8,16},{16,24},{1,9},{9,17},{17,25},{2,10},{10,18},{18,26},{... | collective-permute-start | bytes 24584 | tf_op jit(solution)/shard_map/ppermute | solution.py:19
  67.3 1.3 collective-permute-start.1
  68.6 0.7 fusion.18
  69.3 1.3 iota_compare_fusion
  70.6 1.3 compare_and_fusion.1
  71.9 0.7 sort.17
  72.9 1.3 collective-permute-start.2
  74.2 1.3 collective-permute-start.3
  75.5 3.4 %collective-permute-done.3 = f32[10,1,128]{2,1,0:T(1,128)S(1)} collective-permute-done((f32[10,1,128]{2,1,0:T(1,128)S(1)}, f32[10,1,128]{2,1,0:T(1,128)S(1)}, u32[]{:S(2)}, u32[]{:S(2)}) %collective-permute-start.3) | collective-permute-done | bytes 5152 | tf_op jit(solution)/shard_map/ppermute | solution.py:21
  79.1 3.4 %collective-permute-start.4 = (f32[10,18,1]{2,1,0:T(8,128)S(1)}, f32[10,18,1]{2,1,0:T(8,128)S(1)}, u32[]{:S(2)}, u32[]{:S(2)}) collective-permute-start(f32[10,18,1]{2,1,0:T(8,128)S(1)} %get-tuple-element.196), channel_id=1, source_target_pairs={{0,1},{2,3},{4,5},{6,7},{8,9},{10,11},{12,13},{14,15},{16,17},{18,... | collective-permute-start | bytes 2168 | tf_op jit(solution)/shard_map/ppermute | solution.py:19
  82.5 1.3 collective-permute-start.5
  83.9 1.0 collective-permute-done.4
  84.9 4.5 %collective-permute-done.5 = f32[10,18,1]{2,1,0:T(8,128)S(1)} collective-permute-done((f32[10,18,1]{2,1,0:T(8,128)S(1)}, f32[10,18,1]{2,1,0:T(8,128)S(1)}, u32[]{:S(2)}, u32[]{:S(2)}) %collective-permute-start.5) | collective-permute-done | bytes 752 | tf_op jit(solution)/shard_map/ppermute | solution.py:21
  89.5 0.2 pad_maximum_fusion
  89.7 31.6 %while.29 = (s32[]{:T(128)}, f32[3,16,128]{2,1,0:T(8,128)S(1)}, f32[16,128]{1,0:T(8,128)S(1)}, s32[8]{0:T(128)S(1)}, f32[10,18,130]{2,1,0:T(8,128)S(1)}, /*index...) while((s32[]{:T(128)}, f32[3,16,128]{2,1,0:T(8,128)S(1)}, ...), condition=%wide.region_2.3_spmd.clone, body=%wide.region_1.2_spmd.clone.sunk | while | flops 79883 | bytes 199203 | solution.py:79
  89.7 0.6 dynamic_slice.35
  93.7 0.6 dynamic_slice.35
  97.6 0.6 dynamic_slice.35
  101.6 0.6 dynamic_slice.35
  105.5 0.6 dynamic_slice.35
  109.5 0.6 dynamic_slice.35
  113.4 0.6 dynamic_slice.35
  117.4 0.6 dynamic_slice.35
  121.3 14.8 %all_gather.3 = f32[4,4,16,128]{3,2,1,0:T(8,128)S(1)} all-gather(f32[1,4,16,128]{3,2,1,0:T(8,128)S(1)} %maximum_select_fusion), channel_id=1, replica_groups=mesh['gx'=4,'gy'=4,'gz'=2] {'gx'}, dimensions={0}, use_global_device_ids=true | all-gather | bytes 163840 | tf_op jit(solution)/shard_map/all_gather | solution.py:93
  136.1 0.6 gather_fusion.1
  136.8 0.2 while.30
  137.0 0.6 pad_maximum_fusion.2
  (60 shorter events, 1.7 us)
Async XLA Ops:
  0.0 68.6 %copy-start = (s32[1,1,1,4]{3,2,1,0:T(1,128)S(1)}, s32[1,1,1,4]{3,2,1,0:T(1,128)}, u32[]{:S(2)}) copy-start(s32[1,1,1,4]{3,2,1,0:T(1,128)} %param.11) | copy-start | bytes 52
  0.0 71.8 %copy-start.1 = (s32[4]{0:T(128)S(1)}, s32[4]{0:T(128)}, u32[]{:S(2)}) copy-start(s32[4]{0:T(128)} %param.10) | copy-start | bytes 52
  62.4 10.3 %collective-permute-start = (f32[1,16,128]{2,1,0:T(8,128)S(1)}, f32[1,16,128]{2,1,0:T(8,128)S(1)}, u32[]{:S(2)}, u32[]{:S(2)}) collective-permute-start(f32[1,16,128]{2,1,0:T(8,128)S(1)} %get-tuple-element.194), channel_id=1, source_target_pairs={{0,8},{8,16},{16,24},{1,9},{9,17},{17,25},{2,10},{10,18},{18,26},{... | collective-permute-start | bytes 24584 | tf_op jit(solution)/shard_map/ppermute | solution.py:19
  67.3 5.5 %collective-permute-start.1 = (f32[1,16,128]{2,1,0:T(8,128)S(1)}, f32[1,16,128]{2,1,0:T(8,128)S(1)}, u32[]{:S(2)}, u32[]{:S(2)}) collective-permute-start(f32[1,16,128]{2,1,0:T(8,128)S(1)} %get-tuple-element.195), channel_id=1, source_target_pairs={{8,0},{16,8},{24,16},{9,1},{17,9},{25,17},{10,2},{18,10},{26,18},{... | collective-permute-start | bytes 24584 | tf_op jit(solution)/shard_map/ppermute | solution.py:21
  72.9 2.6 %collective-permute-start.2 = (f32[10,1,128]{2,1,0:T(1,128)S(1)}, f32[10,1,128]{2,1,0:T(1,128)S(1)}, u32[]{:S(2)}, u32[]{:S(2)}) collective-permute-start(f32[10,1,128]{2,1,0:T(1,128)S(1)} %get-tuple-element.198), channel_id=1, source_target_pairs={{0,2},{2,4},{4,6},{1,3},{3,5},{5,7},{8,10},{10,12},{12,14},{9,11},... | collective-permute-start | bytes 15368 | tf_op jit(solution)/shard_map/ppermute | solution.py:19
  74.2 4.8 %collective-permute-start.3 = (f32[10,1,128]{2,1,0:T(1,128)S(1)}, f32[10,1,128]{2,1,0:T(1,128)S(1)}, u32[]{:S(2)}, u32[]{:S(2)}) collective-permute-start(f32[10,1,128]{2,1,0:T(1,128)S(1)} %get-tuple-element.199), channel_id=1, source_target_pairs={{2,0},{4,2},{6,4},{3,1},{5,3},{7,5},{10,8},{12,10},{14,12},{11,9},... | collective-permute-start | bytes 15368 | tf_op jit(solution)/shard_map/ppermute | solution.py:21
  79.1 5.9 %collective-permute-start.4 = (f32[10,18,1]{2,1,0:T(8,128)S(1)}, f32[10,18,1]{2,1,0:T(8,128)S(1)}, u32[]{:S(2)}, u32[]{:S(2)}) collective-permute-start(f32[10,18,1]{2,1,0:T(8,128)S(1)} %get-tuple-element.196), channel_id=1, source_target_pairs={{0,1},{2,3},{4,5},{6,7},{8,9},{10,11},{12,13},{14,15},{16,17},{18,... | collective-permute-start | bytes 2168 | tf_op jit(solution)/shard_map/ppermute | solution.py:19
  82.5 7.0 %collective-permute-start.5 = (f32[10,18,1]{2,1,0:T(8,128)S(1)}, f32[10,18,1]{2,1,0:T(8,128)S(1)}, u32[]{:S(2)}, u32[]{:S(2)}) collective-permute-start(f32[10,18,1]{2,1,0:T(8,128)S(1)} %get-tuple-element.197), channel_id=1, source_target_pairs={{1,0},{3,2},{5,4},{7,6},{9,8},{11,10},{13,12},{15,14},{17,16},{19,... | collective-permute-start | bytes 2168 | tf_op jit(solution)/shard_map/ppermute | solution.py:21
where the time goes:
time: 138 us
  local copies, waits for them, and re-layouts  67 us (49%)
  loops' own time  25.6 us (19%)
  blocking collectives  14.8 us (11%)
  starting transfers between devices  13.6 us (10%)
  waiting for transfers between devices  9.22 us (7%)
  other arithmetic  7.12 us (5%)
    gather x2, local copies, waits for them, and re-layouts, on_device(): looked = jnp.take(transfer_table, volume, axis=1)  59.7 us
    another operation x1, loops' own time, on_device(): lax.scan(advance, start_pair, jnp.arange(slab_depth, dtype=jnp.int32))  25.5 us
    all_gather x1, blocking collectives, on_device(): layers = lax.all_gather(partial_value, 'gx', axis=0, tiled=True)  14.8 us
    ppermute x3, starting transfers between devices, with_halo(): lax.ppermute(tail, axis, [(i, (i + 1) % count) for i in range(ends)])  9.69 us
    ppermute x3, waiting for transfers between devices, with_halo(): lax.ppermute(head, axis, [((i + 1) % count, i) for i in range(ends)])  8.17 us
    dynamic_slice x8, local copies, waits for them, and re-layouts, on_device(): lax.scan(advance, start_pair, jnp.arange(slab_depth, dtype=jnp.int32))  5.09 us
    ppermute x3, starting transfers between devices, with_halo(): lax.ppermute(head, axis, [((i + 1) % count, i) for i in range(ends)])  3.88 us
  transfers between devices with their start and end apart: 6, of which 4 were waited for; matrix products, arithmetic and copies ran while one was open for 3% of the time, Pallas kernels for 0%

commit v1 on v0

v1 whole, which is shorter than its diff:
```python
import functools

import jax
import jax.numpy as jnp
from jax import lax
from jax.experimental import pallas as pl
from jax.experimental.pallas import tpu as pltpu
from jax.sharding import PartitionSpec as P

LIGHT = (1.0 / 3.0, 2.0 / 3.0, 2.0 / 3.0)
AXES = ("gx", "gy", "gz")
MESH = pl.DeviceIdType.MESH


def lookup(table_row, index, lanes):
    entries = table_row.shape[1]
    low = index & (lanes - 1)
    found = None
    for part in range(entries // lanes):
        piece = jnp.broadcast_to(table_row[:, part * lanes:(part + 1) * lanes], index.shape)
        got = jnp.take_along_axis(piece, low, axis=1, mode="promise_in_bounds")
        found = got if found is None else jnp.where(index >= part * lanes, got, found)
    return found


def kernel(sizes, vol_ref, table_ref, rank_ref, foot_ref, out_ref,
           dens, wemit, edge, xh, yh, zh, alphas, colours,
           halo_send, halo_recv, a_send, a_recv, c_send, c_recv):
    n, ny, nz = sizes
    depth, rows, lanes = vol_ref.shape
    extent = 4.0 / (depth * n)
    me = [lax.axis_index(a) for a in AXES]
    ix = me[0]

    barrier = pltpu.get_barrier_semaphore()
    for off in range(1, n):
        pl.semaphore_signal(barrier, inc=1, device_id={"gx": lax.rem(ix + off, n)}, device_id_type=MESH)
    for a in (1, 2):
        if sizes[a] > 1:
            @pl.when(me[a] > 0)
            def _():
                pl.semaphore_signal(barrier, inc=1, device_id={AXES[a]: me[a] - 1}, device_id_type=MESH)

            @pl.when(me[a] < sizes[a] - 1)
            def _():
                pl.semaphore_signal(barrier, inc=1, device_id={AXES[a]: me[a] + 1}, device_id_type=MESH)

    lane = lax.broadcasted_iota(jnp.int32, (8, lanes), 1)
    vol = vol_ref[...].reshape(depth * rows, lanes)
    d_all = lookup(table_ref[3:4, :], vol, lanes)
    d3 = d_all.reshape(depth, rows, lanes)
    dens[...] = d3
    edge[0] = d3[:, 0, :]
    edge[1] = d3[:, rows - 1, :]
    first = jnp.zeros((8, lanes), jnp.float32)
    last = jnp.zeros((8, lanes), jnp.float32)
    groups = depth * rows // 8
    for v in range(groups):
        piece = d_all[v * 8:(v + 1) * 8]
        to_last = (2 * v + 1) % lanes
        to_first = (2 * v - 1) % lanes
        last = jnp.where(lane == 2 * v, pltpu.roll(piece, to_last, 1) if to_last else piece, last)
        first = jnp.where(lane == to_first, pltpu.roll(piece, to_first, 1) if to_first else piece, first)
    edge[2] = first
    edge[3] = last

    sources = (
        (dens.at[0], dens.at[depth - 1]),
        (edge.at[0], edge.at[1]),
        (edge.at[2], edge.at[3]),
    )
    halos = (xh, yh, zh)

    def halo_copy(a, upward):
        slot = 0 if upward else 1
        return pltpu.make_async_remote_copy(
            src_ref=sources[a][1 if upward else 0],
            dst_ref=halos[a].at[slot],
            send_sem=halo_send.at[a, slot],
            recv_sem=halo_recv.at[a, slot],
            device_id={AXES[a]: me[a] + (1 if upward else -1)},
            device_id_type=MESH,
        )

    greeted = n - 1
    for a in (1, 2):
        greeted = greeted + lax.min(me[a], 1) + lax.min(sizes[a] - 1 - me[a], 1)
    pl.semaphore_wait(barrier, greeted)

    for a in range(3):
        @pl.when(me[a] < sizes[a] - 1)
        def _():
            halo_copy(a, True).start()

        @pl.when(me[a] == 0)
        def _():
            halos[a][0] = jnp.zeros(halos[a].shape[1:], jnp.float32)

        @pl.when(me[a] > 0)
        def _():
            halo_copy(a, False).start()

        @pl.when(me[a] == sizes[a] - 1)
        def _():
            halos[a][1] = jnp.zeros(halos[a].shape[1:], jnp.float32)

    row_no = lax.broadcasted_iota(jnp.int32, (rows, lanes), 0)
    lane_no = lax.broadcasted_iota(jnp.int32, (rows, lanes), 1)
    inside = (
        (row_no >= foot_ref[0, 0, 0, 0])
        & (row_no < foot_ref[0, 0, 0, 1])
        & (lane_no >= foot_ref[0, 0, 0, 2])
        & (lane_no < foot_ref[0, 0, 0, 3])
    )

    transmit = jnp.ones((rows, lanes), jnp.float32)
    weights = []
    for x in range(depth):
        sample = 1.0 - jnp.exp(-extent * d3[x])
        weights.append(transmit * sample)
        transmit = transmit * (1.0 - sample)
    alphas[ix] = jnp.where(inside, 1.0 - transmit, 0.0)

    def image_copy(buf, off, s_sem, r_sem):
        return pltpu.make_async_remote_copy(
            src_ref=buf.at[ix],
            dst_ref=buf.at[ix],
            send_sem=s_sem.at[off],
            recv_sem=r_sem.at[off],
            device_id={"gx": lax.rem(ix + off, n)},
            device_id_type=MESH,
        )

    for off in range(n - 1, 0, -1):
        image_copy(alphas, off, a_send, a_recv).start()

    for c in range(3):
        emit = lookup(table_ref[c:c + 1, :], vol, lanes).reshape(depth, rows, lanes)
        for x in range(depth):
            wemit[c, x] = weights[x] * emit[x]

    for a in range(3):
        @pl.when(me[a] > 0)
        def _():
            halo_copy(a, True).wait_recv()

        @pl.when(me[a] < sizes[a] - 1)
        def _():
            halo_copy(a, False).wait_recv()

    sides = zh[0] + zh[1]
    layers = [xh[0]] + [dens[x] for x in range(depth)] + [xh[1]]
    colour = [jnp.zeros((rows, lanes), jnp.float32) for _ in range(3)]
    per = rows // 8
    for x in range(depth):
        d = layers[x + 1]
        g_x = 0.5 * (layers[x + 2] - layers[x])
        up = jnp.where(row_no == 0, yh[0, x:x + 1, :], pltpu.roll(d, 1, 0))
        down = jnp.where(row_no == rows - 1, yh[1, x:x + 1, :], pltpu.roll(d, rows - 1, 0))
        g_y = 0.5 * (down - up)
        pieces = []
        for h in range(per):
            v = x * per + h
            pieces.append(pltpu.roll(sides, (lanes - 2 * v) % lanes, 1) if v else sides)
        side = jnp.concatenate(pieces, axis=0)
        left = jnp.where(lane_no == 0, side, pltpu.roll(d, 1, 1))
        right = jnp.where(lane_no == lanes - 1, side, pltpu.roll(d, lanes - 1, 1))
        g_z = 0.5 * (right - left)
        facing = jnp.abs(g_x * LIGHT[0] + g_y * LIGHT[1] + g_z * LIGHT[2]) * lax.rsqrt(
            1.0 + (g_x * g_x + g_y * g_y + g_z * g_z)
        )
        shade = 0.35 + 0.65 * facing
        for c in range(3):
            colour[c] = colour[c] + wemit[c, x] * shade
    for c in range(3):
        colours[ix, c] = jnp.where(inside, colour[c], 0.0)

    for off in range(n - 1, 0, -1):
        image_copy(colours, off, c_send, c_recv).start()

    order = []
    for p in range(n):
        at = 0
        for i in range(n):
            at = jnp.where(rank_ref[i] == p, i, at)
        order.append(at)

    for off in range(1, n):
        image_copy(alphas, off, a_send, a_recv).wait_recv()
    for off in range(1, n):
        image_copy(colours, off, c_send, c_recv).wait_recv()

    total = [jnp.zeros((rows, lanes), jnp.float32) for _ in range(4)]
    for p in range(n):
        cover = 1.0 - total[3]
        for c in range(3):
            total[c] = total[c] + cover * colours[order[p], c]
        total[3] = total[3] + cover * alphas[order[p]]
    for c in range(4):
        out_ref[c] = total[c]

    for a in range(3):
        @pl.when(me[a] < sizes[a] - 1)
        def _():
            halo_copy(a, True).wait_send()

        @pl.when(me[a] > 0)
        def _():
            halo_copy(a, False).wait_send()
    for off in range(1, n):
        image_copy(alphas, off, a_send, a_recv).wait_send()
        image_copy(colours, off, c_send, c_recv).wait_send()


def on_device(sizes, volume, transfer_table, depth_rank, footprint):
    depth, rows, lanes = volume.shape
    n = sizes[0]
    vmem = pl.BlockSpec(memory_space=pltpu.VMEM)
    smem = pl.BlockSpec(memory_space=pltpu.SMEM)
    return pl.pallas_call(
        functools.partial(kernel, sizes),
        out_shape=jax.ShapeDtypeStruct((4, rows, lanes), jnp.float32),
        in_specs=[vmem, vmem, smem, smem],
        out_specs=vmem,
        scratch_shapes=[
            pltpu.VMEM((depth, rows, lanes), jnp.float32),
            pltpu.VMEM((3, depth, rows, lanes), jnp.float32),
            pltpu.VMEM((4, 8, lanes), jnp.float32),
            pltpu.VMEM((2, rows, lanes), jnp.float32),
            pltpu.VMEM((2, depth, lanes), jnp.float32),
            pltpu.VMEM((2, 8, lanes), jnp.float32),
            pltpu.VMEM((n, rows, lanes), jnp.float32),
            pltpu.VMEM((n, 3, rows, lanes), jnp.float32),
            pltpu.SemaphoreType.DMA((3, 2)),
            pltpu.SemaphoreType.DMA((3, 2)),
            pltpu.SemaphoreType.DMA((n,)),
            pltpu.SemaphoreType.DMA((n,)),
            pltpu.SemaphoreType.DMA((n,)),
            pltpu.SemaphoreType.DMA((n,)),
        ],
        compiler_params=pltpu.CompilerParams(collective_id=0, has_side_effects=True),
        name="raycast",
    )(volume, transfer_table, depth_rank, footprint)


def solution(mesh):
    placed = (P("gx", "gy", "gz"), P(), P(), P("gx", "gy", "gz", None))
    sizes = tuple(mesh.shape[a] for a in AXES)
    return jax.shard_map(
        functools.partial(on_device, sizes), mesh=mesh, in_specs=placed,
        out_specs=P(None, "gy", "gz"), check_vma=False,
    )
```

time: 138 us -> 15.4 us (0.11)
  local copies, waits for them, and re-layouts: 67 us -> 1.38 us
  loops' own time: 25.6 us -> 0 us
  blocking collectives: 14.8 us -> 0 us
  Pallas kernels: 0 us -> 13.8 us
  starting transfers between devices: 13.6 us -> 0 us
  waiting for transfers between devices: 9.22 us -> 0 us
  other arithmetic: 7.12 us -> 0 us
    gather x3 -> x0, local copies, waits for them, and re-layouts: 60.3 us -> none  [the longest x2 59.7 us: on_device(): looked = jnp.take(transfer_table, volume, axis=1)]
    another operation x2 -> x0, loops' own time: 25.6 us -> none  [the longest x1 25.5 us: on_device(): lax.scan(advance, start_pair, jnp.arange(slab_depth, dtype=jnp.int32))]
    all_gather x1 -> x0, blocking collectives: 14.8 us -> none  [on_device(): layers = lax.all_gather(partial_value, 'gx', axis=0, tiled=True)]
    pallas_call x0 -> x1, Pallas kernels: none -> 13.8 us  [on_device(): pl.pallas_call(functools.partial(kernel, sizes), out_shape=jax.ShapeDtype...]
    ppermute x6 -> x0, starting transfers between devices: 13.6 us -> none  [the longest x3 9.69 us: with_halo(): lax.ppermute(tail, axis, [(i, (i + 1) % count) for i in range(ends)])]
    ppermute x6 -> x0, waiting for transfers between devices: 9.22 us -> none  [the longest x3 8.17 us: with_halo(): lax.ppermute(head, axis, [((i + 1) % count, i) for i in range(ends)])]
    dynamic_slice x8 -> x0, local copies, waits for them, and re-layouts: 5.09 us -> none  [on_device(): lax.scan(advance, start_pair, jnp.arange(slab_depth, dtype=jnp.int32))]
    and x4 -> x0, other arithmetic: 2.22 us -> none  [the longest x2 1.35 us: on_device(): (rows_local >= rect[0]) & (rows_local < rect[1]) & (cols_local >= rect[2])]
  transfers between devices with their start and end apart: 6 -> 0, of which waited for: 4 -> 0; matrix products, arithmetic and copies ran while one was open for 3% -> 0% of each run, Pallas kernels for 0% -> 0%
where the time goes in v1:
time: 15.4 us; the launch traced here: 15.2 us
  Pallas kernels  13.8 us (90%)
  local copies, waits for them, and re-layouts  1.38 us (9%)
    pallas_call x1, Pallas kernels, on_device(): pl.pallas_call(functools.partial(kernel, sizes), out_shape=jax.ShapeDtype...  13.8 us
    unnamed x1, local copies, waits for them, and re-layouts  1.38 us

profile of v1, /device:TPU:0, one launch (start us, length us, event | category | flops | bytes accessed | tf_op | source)
XLA Modules:
  0.0 15.2 jit_solution(473071625420328519)
XLA Ops:
  0.0 13.8 %raycast.1 = f32[4,16,128]{2,1,0:T(8,128)} custom-call(s32[8,16,128]{2,1,0:T(8,128)} %vol_ref.1, f32[4,256]{1,0:T(4,128)} %table_ref.1, s32[4]{0:T(128)} %rank_ref.1, s32[1,1,1,4]{3,2,1,0:T(1,128)} %foot_ref.1), custom_call_target="tpu_custom_call" | custom-call | tf_op jit(solution)/shard_map/raycast/pallas_call | solution.py:220
  13.8 1.4 %copy.6 = f32[4,16,128]{2,1,0:T(8,128)} copy(f32[4,16,128]{2,1,0:T(8,128)} %raycast.1) | data formatting | bytes 65536

commit v2 on v1

--- a/solution.py
+++ b/solution.py
@@ -23,8 +23,8 @@
     return found
 
 
-def kernel(sizes, vol_ref, table_ref, rank_ref, foot_ref, out_ref,
-           dens, wemit, edge, xh, yh, zh, alphas, colours,
+def kernel(sizes, vol_hbm, table_hbm, rank_hbm, foot_hbm, out_ref,
+           vol_ref, table_ref, rank_ref, foot_ref, load_sem, dens, wemit, edge, xh, yh, zh, alphas, colours,
            halo_send, halo_recv, a_send, a_recv, c_send, c_recv):
     n, ny, nz = sizes
     depth, rows, lanes = vol_ref.shape
@@ -44,6 +44,17 @@
             @pl.when(me[a] < sizes[a] - 1)
             def _():
                 pl.semaphore_signal(barrier, inc=1, device_id={AXES[a]: me[a] + 1}, device_id_type=MESH)
+
+    loads = [
+        pltpu.make_async_copy(src, dst, load_sem.at[i])
+        for i, (src, dst) in enumerate((
+            (vol_hbm, vol_ref), (table_hbm, table_ref), (foot_hbm, foot_ref), (rank_hbm, rank_ref)
+        ))
+    ]
+    for load in loads:
+        load.start()
+    loads[0].wait()
+    loads[1].wait()
 
     lane = lax.broadcasted_iota(jnp.int32, (8, lanes), 1)
     vol = vol_ref[...].reshape(depth * rows, lanes)
@@ -104,6 +115,7 @@
         def _():
             halos[a][1] = jnp.zeros(halos[a].shape[1:], jnp.float32)
 
+    loads[2].wait()
     row_no = lax.broadcasted_iota(jnp.int32, (rows, lanes), 0)
     lane_no = lax.broadcasted_iota(jnp.int32, (rows, lanes), 1)
     inside = (
@@ -131,8 +143,17 @@
             device_id_type=MESH,
         )
 
-    for off in range(n - 1, 0, -1):
-        image_copy(alphas, off, a_send, a_recv).start()
+    def send_images(buf, s_sem, r_sem):
+        for far in range(n - 1, 0, -1):
+            @pl.when(ix + far < n)
+            def _():
+                image_copy(buf, far, s_sem, r_sem).start()
+
+            @pl.when(ix - far >= 0)
+            def _():
+                image_copy(buf, n - far, s_sem, r_sem).start()
+
+    send_images(alphas, a_send, a_recv)
 
     for c in range(3):
         emit = lookup(table_ref[c:c + 1, :], vol, lanes).reshape(depth, rows, lanes)
@@ -175,9 +196,9 @@
     for c in range(3):
         colours[ix, c] = jnp.where(inside, colour[c], 0.0)
 
-    for off in range(n - 1, 0, -1):
-        image_copy(colours, off, c_send, c_recv).start()
-
+    send_images(colours, c_send, c_recv)
+
+    loads[3].wait()
     order = []
     for p in range(n):
         at = 0
@@ -216,13 +237,18 @@
     depth, rows, lanes = volume.shape
     n = sizes[0]
     vmem = pl.BlockSpec(memory_space=pltpu.VMEM)
-    smem = pl.BlockSpec(memory_space=pltpu.SMEM)
+    hbm = pl.BlockSpec(memory_space=pl.ANY)
     return pl.pallas_call(
         functools.partial(kernel, sizes),
         out_shape=jax.ShapeDtypeStruct((4, rows, lanes), jnp.float32),
-        in_specs=[vmem, vmem, smem, smem],
+        in_specs=[hbm] * 4,
         out_specs=vmem,
         scratch_shapes=[
+            pltpu.VMEM(volume.shape, jnp.int32),
+            pltpu.VMEM(transfer_table.shape, jnp.float32),
+            pltpu.SMEM(depth_rank.shape, jnp.int32),
+            pltpu.SMEM(footprint.shape, jnp.int32),
+            pltpu.SemaphoreType.DMA((4,)),
             pltpu.VMEM((depth, rows, lanes), jnp.float32),
             pltpu.VMEM((3, depth, rows, lanes), jnp.float32),
             pltpu.VMEM((4, 8, lanes), jnp.float32),

time: 15.4 us -> 14.1 us (0.916)
  Pallas kernels: 13.8 us -> 12.5 us
    pallas_call x1, Pallas kernels: 13.8 us -> 12.5 us  [on_device(): pl.pallas_call(functools.partial(kernel, sizes), out_shape=jax.ShapeDtype...]
where the time goes in v2:
time: 14.1 us; the launch traced here: 13.9 us
  Pallas kernels  12.5 us (89%)
  local copies, waits for them, and re-layouts  1.38 us (10%)
    pallas_call x1, Pallas kernels, on_device(): pl.pallas_call(functools.partial(kernel, sizes), out_shape=jax.ShapeDtype...  12.5 us
    unnamed x1, local copies, waits for them, and re-layouts  1.38 us

profile of v2, /device:TPU:0, one launch (start us, length us, event | category | flops | bytes accessed | tf_op | source)
XLA Modules:
  0.0 13.9 jit_solution(16931462738092540009)
XLA Ops:
  0.0 12.5 %raycast.1 = f32[4,16,128]{2,1,0:T(8,128)} custom-call(s32[8,16,128]{2,1,0:T(8,128)} %vol_hbm.1, f32[4,256]{1,0:T(4,128)} %table_hbm.1, s32[4]{0:T(128)} %rank_hbm.1, s32[1,1,1,4]{3,2,1,0:T(1,128)} %foot_hbm.1), custom_call_target="tpu_custom_call" | custom-call | tf_op jit(solution)/shard_map/raycast/pallas_call | solution.py:241
  12.5 1.4 %copy.6 = f32[4,16,128]{2,1,0:T(8,128)} copy(f32[4,16,128]{2,1,0:T(8,128)} %raycast.1) | data formatting | bytes 65536

commit v3 on v2

--- a/solution.py
+++ b/solution.py
@@ -240,7 +240,7 @@
     hbm = pl.BlockSpec(memory_space=pl.ANY)
     return pl.pallas_call(
         functools.partial(kernel, sizes),
-        out_shape=jax.ShapeDtypeStruct((4, rows, lanes), jnp.float32),
+        out_shape=pltpu.VMEM((4, rows, lanes), jnp.float32),
         in_specs=[hbm] * 4,
         out_specs=vmem,
         scratch_shapes=[

time: 14.1 us -> 12.7 us (0.901)
  local copies, waits for them, and re-layouts: 1.38 us -> 0.62 us
  Pallas kernels: 12.5 us -> 11.9 us
    unnamed x1, local copies, waits for them, and re-layouts: 1.38 us -> 0.62 us
    pallas_call x1, Pallas kernels: 12.5 us -> 11.9 us  [on_device(): pl.pallas_call(functools.partial(kernel, sizes), out_shape=pltpu.VMEM((4,...]
where the time goes in v3:
time: 12.7 us; the launch traced here: 12.5 us
  Pallas kernels  11.9 us (94%)
  local copies, waits for them, and re-layouts  0.62 us (5%)
    pallas_call x1, Pallas kernels, on_device(): pl.pallas_call(functools.partial(kernel, sizes), out_shape=pltpu.VMEM((4,...  11.9 us
    unnamed x1, local copies, waits for them, and re-layouts  0.62 us

profile of v3, /device:TPU:0, one launch (start us, length us, event | category | flops | bytes accessed | tf_op | source)
XLA Modules:
  0.0 12.5 jit_solution(4595652714768500583)
XLA Ops:
  0.0 11.9 %raycast.1 = f32[4,16,128]{2,1,0:T(8,128)S(1)} custom-call(s32[8,16,128]{2,1,0:T(8,128)} %vol_hbm.1, f32[4,256]{1,0:T(4,128)} %table_hbm.1, s32[4]{0:T(128)} %rank_hbm.1, s32[1,1,1,4]{3,2,1,0:T(1,128)} %foot_hbm.1), custom_call_target="tpu_custom_call" | custom-call | tf_op jit(solution)/shard_map/raycast/pallas_call | solution.py:241
  11.9 0.6 %copy.6 = f32[4,16,128]{2,1,0:T(8,128)} copy(f32[4,16,128]{2,1,0:T(8,128)S(1)} %raycast.1) | data formatting | bytes 65536

commit v4 on v3

--- a/solution.py
+++ b/solution.py
@@ -24,7 +24,7 @@
 
 
 def kernel(sizes, vol_hbm, table_hbm, rank_hbm, foot_hbm, out_ref,
-           vol_ref, table_ref, rank_ref, foot_ref, load_sem, dens, wemit, edge, xh, yh, zh, alphas, colours,
+           vol_ref, table_ref, rank_ref, foot_ref, load_sem, dens, wemit, inner, edge, xh, yh, zh, alphas, colours,
            halo_send, halo_recv, a_send, a_recv, c_send, c_recv):
     n, ny, nz = sizes
     depth, rows, lanes = vol_ref.shape
@@ -98,7 +98,7 @@
         greeted = greeted + lax.min(me[a], 1) + lax.min(sizes[a] - 1 - me[a], 1)
     pl.semaphore_wait(barrier, greeted)
 
-    for a in range(3):
+    for a in (1, 2, 0):
         @pl.when(me[a] < sizes[a] - 1)
         def _():
             halo_copy(a, True).start()
@@ -160,6 +160,18 @@
         for x in range(depth):
             wemit[c, x] = weights[x] * emit[x]
 
+    per = rows // 8
+    for x in range(depth):
+        d = d3[x]
+        up = jnp.where(row_no == 0, 0.0, pltpu.roll(d, 1, 0))
+        down = jnp.where(row_no == rows - 1, 0.0, pltpu.roll(d, rows - 1, 0))
+        inner[0, x] = 0.5 * (down - up)
+        left = jnp.where(lane_no == 0, 0.0, pltpu.roll(d, 1, 1))
+        right = jnp.where(lane_no == lanes - 1, 0.0, pltpu.roll(d, lanes - 1, 1))
+        inner[1, x] = 0.5 * (right - left)
+    line = lax.broadcasted_iota(jnp.int32, (8, lanes), 0)
+    on_side = (lane == 0) | (lane == lanes - 1)
+
     for a in range(3):
         @pl.when(me[a] > 0)
         def _():
@@ -169,30 +181,32 @@
         def _():
             halo_copy(a, False).wait_recv()
 
-    sides = zh[0] + zh[1]
-    layers = [xh[0]] + [dens[x] for x in range(depth)] + [xh[1]]
-    colour = [jnp.zeros((rows, lanes), jnp.float32) for _ in range(3)]
-    per = rows // 8
+    sides = 0.5 * (zh[1] - zh[0])
+    half_up = 0.5 * yh[0]
+    half_down = 0.5 * yh[1]
+    layers = [xh.at[0]] + [dens.at[x] for x in range(depth)] + [xh.at[1]]
+    colour = [[None] * per for _ in range(3)]
     for x in range(depth):
-        d = layers[x + 1]
-        g_x = 0.5 * (layers[x + 2] - layers[x])
-        up = jnp.where(row_no == 0, yh[0, x:x + 1, :], pltpu.roll(d, 1, 0))
-        down = jnp.where(row_no == rows - 1, yh[1, x:x + 1, :], pltpu.roll(d, rows - 1, 0))
-        g_y = 0.5 * (down - up)
-        pieces = []
         for h in range(per):
+            at = pl.ds(h * 8, 8)
             v = x * per + h
-            pieces.append(pltpu.roll(sides, (lanes - 2 * v) % lanes, 1) if v else sides)
-        side = jnp.concatenate(pieces, axis=0)
-        left = jnp.where(lane_no == 0, side, pltpu.roll(d, 1, 1))
-        right = jnp.where(lane_no == lanes - 1, side, pltpu.roll(d, lanes - 1, 1))
-        g_z = 0.5 * (right - left)
-        facing = jnp.abs(g_x * LIGHT[0] + g_y * LIGHT[1] + g_z * LIGHT[2]) * lax.rsqrt(
-            1.0 + (g_x * g_x + g_y * g_y + g_z * g_z)
-        )
-        shade = 0.35 + 0.65 * facing
-        for c in range(3):
-            colour[c] = colour[c] + wemit[c, x] * shade
+            g_x = 0.5 * (layers[x + 2][at, :] - layers[x][at, :])
+            g_y = inner[0, x, at, :]
+            if h == 0:
+                g_y = jnp.where(line == 0, g_y - half_up[x:x + 1, :], g_y)
+            if h == per - 1:
+                g_y = jnp.where(line == 7, g_y + half_down[x:x + 1, :], g_y)
+            side = pltpu.roll(sides, lanes - 2 * v, 1) if v else sides
+            g_z = inner[1, x, at, :]
+            g_z = jnp.where(on_side, g_z + side, g_z)
+            facing = jnp.abs(g_x * LIGHT[0] + g_y * LIGHT[1] + g_z * LIGHT[2]) * lax.rsqrt(
+                1.0 + (g_x * g_x + g_y * g_y + g_z * g_z)
+            )
+            shade = 0.35 + 0.65 * facing
+            for c in range(3):
+                term = wemit[c, x, at, :] * shade
+                colour[c][h] = term if x == 0 else colour[c][h] + term
+    colour = [jnp.concatenate(c, axis=0) for c in colour]
     for c in range(3):
         colours[ix, c] = jnp.where(inside, colour[c], 0.0)
 
@@ -208,18 +222,12 @@
 
     for off in range(1, n):
         image_copy(alphas, off, a_send, a_recv).wait_recv()
-    for off in range(1, n):
-        image_copy(colours, off, c_send, c_recv).wait_recv()
-
-    total = [jnp.zeros((rows, lanes), jnp.float32) for _ in range(4)]
+    covers = []
+    alpha = jnp.zeros((rows, lanes), jnp.float32)
     for p in range(n):
-        cover = 1.0 - total[3]
-        for c in range(3):
-            total[c] = total[c] + cover * colours[order[p], c]
-        total[3] = total[3] + cover * alphas[order[p]]
-    for c in range(4):
-        out_ref[c] = total[c]
-
+        covers.append(1.0 - alpha)
+        alpha = alpha + covers[p] * alphas[order[p]]
+    out_ref[3] = alpha
     for a in range(3):
         @pl.when(me[a] < sizes[a] - 1)
         def _():
@@ -230,6 +238,17 @@
             halo_copy(a, False).wait_send()
     for off in range(1, n):
         image_copy(alphas, off, a_send, a_recv).wait_send()
+
+    for off in range(1, n):
+        image_copy(colours, off, c_send, c_recv).wait_recv()
+    total = [None] * 3
+    for p in range(n):
+        for c in range(3):
+            term = covers[p] * colours[order[p], c]
+            total[c] = term if p == 0 else total[c] + term
+    for c in range(3):
+        out_ref[c] = total[c]
+    for off in range(1, n):
         image_copy(colours, off, c_send, c_recv).wait_send()
 
 
@@ -251,6 +270,7 @@
             pltpu.SemaphoreType.DMA((4,)),
             pltpu.VMEM((depth, rows, lanes), jnp.float32),
             pltpu.VMEM((3, depth, rows, lanes), jnp.float32),
+            pltpu.VMEM((2, depth, rows, lanes), jnp.float32),
             pltpu.VMEM((4, 8, lanes), jnp.float32),
             pltpu.VMEM((2, rows, lanes), jnp.float32),
             pltpu.VMEM((2, depth, lanes), jnp.float32),

time: 12.7 us -> 12.6 us (level)
  no operation moved by 1% of the time
where the time goes in v4:
time: 12.6 us; the launch traced here: 12.5 us
  Pallas kernels  11.8 us (94%)
  local copies, waits for them, and re-layouts  0.62 us (5%)
    pallas_call x1, Pallas kernels, on_device(): pl.pallas_call(functools.partial(kernel, sizes), out_shape=pltpu.VMEM((4,...  11.8 us
    unnamed x1, local copies, waits for them, and re-layouts  0.62 us

profile of v4, /device:TPU:0, one launch (start us, length us, event | category | flops | bytes accessed | tf_op | source)
XLA Modules:
  0.0 12.5 jit_solution(15786446881382230854)
XLA Ops:
  0.0 11.8 %raycast.1 = f32[4,16,128]{2,1,0:T(8,128)S(1)} custom-call(s32[8,16,128]{2,1,0:T(8,128)} %vol_hbm.1, f32[4,256]{1,0:T(4,128)} %table_hbm.1, s32[4]{0:T(128)} %rank_hbm.1, s32[1,1,1,4]{3,2,1,0:T(1,128)} %foot_hbm.1), custom_call_target="tpu_custom_call" | custom-call | tf_op jit(solution)/shard_map/raycast/pallas_call | solution.py:260
  11.9 0.6 %copy.6 = f32[4,16,128]{2,1,0:T(8,128)} copy(f32[4,16,128]{2,1,0:T(8,128)S(1)} %raycast.1) | data formatting | bytes 65536

commit v5 on v4

--- a/solution.py
+++ b/solution.py
@@ -93,23 +93,10 @@
             device_id_type=MESH,
         )
 
-    greeted = n - 1
-    for a in (1, 2):
-        greeted = greeted + lax.min(me[a], 1) + lax.min(sizes[a] - 1 - me[a], 1)
-    pl.semaphore_wait(barrier, greeted)
-
-    for a in (1, 2, 0):
-        @pl.when(me[a] < sizes[a] - 1)
-        def _():
-            halo_copy(a, True).start()
-
+    for a in range(3):
         @pl.when(me[a] == 0)
         def _():
             halos[a][0] = jnp.zeros(halos[a].shape[1:], jnp.float32)
-
-        @pl.when(me[a] > 0)
-        def _():
-            halo_copy(a, False).start()
 
         @pl.when(me[a] == sizes[a] - 1)
         def _():
@@ -132,6 +119,20 @@
         weights.append(transmit * sample)
         transmit = transmit * (1.0 - sample)
     alphas[ix] = jnp.where(inside, 1.0 - transmit, 0.0)
+
+    greeted = n - 1
+    for a in (1, 2):
+        greeted = greeted + lax.min(me[a], 1) + lax.min(sizes[a] - 1 - me[a], 1)
+    pl.semaphore_wait(barrier, greeted)
+
+    for a in (1, 2, 0):
+        @pl.when(me[a] < sizes[a] - 1)
+        def _():
+            halo_copy(a, True).start()
+
+        @pl.when(me[a] > 0)
+        def _():
+            halo_copy(a, False).start()
 
     def image_copy(buf, off, s_sem, r_sem):
         return pltpu.make_async_remote_copy(

time: 12.6 us -> 12.7 us (level)
  no operation moved by 1% of the time
where the time goes in v5:
time: 12.7 us; the launch traced here: 12.5 us
  Pallas kernels  11.9 us (94%)
  local copies, waits for them, and re-layouts  0.62 us (5%)
    pallas_call x1, Pallas kernels, on_device(): pl.pallas_call(functools.partial(kernel, sizes), out_shape=pltpu.VMEM((4,...  11.9 us
    unnamed x1, local copies, waits for them, and re-layouts  0.62 us

profile of v5, /device:TPU:0, one launch (start us, length us, event | category | flops | bytes accessed | tf_op | source)
XLA Modules:
  0.0 12.5 jit_solution(4600960984569596568)
XLA Ops:
  0.0 11.9 %raycast.1 = f32[4,16,128]{2,1,0:T(8,128)S(1)} custom-call(s32[8,16,128]{2,1,0:T(8,128)} %vol_hbm.1, f32[4,256]{1,0:T(4,128)} %table_hbm.1, s32[4]{0:T(128)} %rank_hbm.1, s32[1,1,1,4]{3,2,1,0:T(1,128)} %foot_hbm.1), custom_call_target="tpu_custom_call" | custom-call | tf_op jit(solution)/shard_map/raycast/pallas_call | solution.py:261
  11.9 0.6 %copy.6 = f32[4,16,128]{2,1,0:T(8,128)} copy(f32[4,16,128]{2,1,0:T(8,128)S(1)} %raycast.1) | data formatting | bytes 65536
